TPU v7x, 8 devices: a whole 2x2x1 slice. The times are simulated.
8 devices in a mesh: dp: 2 (over z, y), tp: 4 (over x, core).
Axes of the slice: x: 2, y: 2, z: 1, core: 2. Of those that a mesh axis runs over, the one named last changes fastest.
Arguments:
- query: bfloat16 [128, 28, 128], P('dp', 'tp'), parts along dimension 0
- k_cache: bfloat16 [128, 2048, 4, 128], P('dp', None, 'tp'), parts along dimension 0
- v_cache: bfloat16 [128, 2048, 4, 128], P('dp', None, 'tp'), parts along dimension 0
- k_new: bfloat16 [128, 4, 128], P('dp', 'tp'), parts along dimension 0
- v_new: bfloat16 [128, 4, 128], P('dp', 'tp'), parts along dimension 0
- lens: int32 [128], P('dp'), parts along dimension 0
Outputs:
- output 1: bfloat16 [128, 28, 128], P('dp', 'tp'), parts along dimension 0
- output 2: bfloat16 [128, 2048, 4, 128], P('dp', 'tp'), parts along dimension 0
- output 3: bfloat16 [128, 2048, 4, 128], P('dp', 'tp'), parts along dimension 0
There are 2 independent parts. A program takes and returns all parts, laid end to end along the dimension named above; each array names one.
All inputs are finite; a program needn't handle non-finite values.
Results may differ from a plain program's by a relative error of at most 0.00775914.
Values are sent between devices in bfloat16 or wider.
A program may use at most 1 GiB of HBM per device.

v0:
```python
import jax
import jax.numpy as jnp
from jax import lax
from jax.sharding import PartitionSpec as P

MASK_VALUE = -1e30


def solution(mesh):
    def local_step(query, k_cache, v_cache, k_new, v_new, lens):
        batch, seq_len, head_dim = k_cache.shape[0], k_cache.shape[1], k_cache.shape[3]
        positions = lax.broadcasted_iota(jnp.int32, (1, seq_len, 1, 1), 1)
        new_slot = positions == lens[:, None, None, None]
        k_upd = jnp.where(new_slot, k_new[:, None], k_cache)
        v_upd = jnp.where(new_slot, v_new[:, None], v_cache)
        k_seq = lax.all_to_all(k_upd, "tp", 1, 2, tiled=True)
        v_seq = lax.all_to_all(v_upd, "tp", 1, 2, tiled=True)
        q_all = lax.all_gather(query, "tp", axis=1, tiled=True)
        seq_local, kv_heads = k_seq.shape[1], k_seq.shape[2]
        q_heads = q_all.shape[1]
        q_grp = q_all.reshape(batch, kv_heads, q_heads // kv_heads, head_dim)
        scores = jnp.einsum("bhgd,bthd->bhgt", q_grp, k_seq, preferred_element_type=jnp.float32) * (head_dim ** -0.5)
        tok_pos = lax.axis_index("tp") * seq_local + lax.broadcasted_iota(jnp.int32, (1, 1, 1, seq_local), 3)
        valid = tok_pos <= lens[:, None, None, None]
        scores = jnp.where(valid, scores, MASK_VALUE)
        part_max = jnp.max(scores, axis=-1)
        weights = jnp.where(valid, jnp.exp(scores - part_max[..., None]), 0.0)
        part_sum = jnp.sum(weights, axis=-1)
        part_out = jnp.einsum("bhgt,bthd->bhgd", weights.astype(jnp.bfloat16), v_seq, preferred_element_type=jnp.float32)
        glob_max = lax.pmax(part_max, "tp")
        factor = jnp.exp(part_max - glob_max)
        stacked = jnp.concatenate([part_out * factor[..., None], (part_sum * factor)[..., None]], axis=-1)
        stacked = stacked.reshape(batch, q_heads, head_dim + 1)
        own_heads = lax.psum_scatter(stacked, "tp", scatter_dimension=1, tiled=True)
        attn_out = (own_heads[..., :head_dim] / own_heads[..., head_dim:]).astype(jnp.bfloat16)
        return attn_out, k_seq, v_seq

    head_spec = P("dp", "tp")
    entry_spec = P("dp", None, "tp")
    return jax.shard_map(local_step, mesh=mesh, in_specs=(head_spec, entry_spec, entry_spec, head_spec, head_spec, P("dp")), out_specs=(head_spec, P("dp", "tp"), P("dp", "tp")), check_vma=False)
```

profile of v0, /device:TPU:0, one launch (start us, length us, event | category | flops | bytes accessed | tf_op | source)
XLA Modules:
  0.0 1019.3 jit_solution(12628953500025992463)
XLA Ops:
  7.2 0.8 iota_compare_fusion
  8.0 60.5 %copy_select_fusion = (bf16[64,2048,1,128]{3,0,2,1:T(8,128)(2,1)}, bf16[64,2048,1,128]{3,0,2,1:T(8,128)(2,1)}) fusion(bf16[64,2048,1,128]{3,1,2,0:T(8,128)(2,1)} %param.8, pred[64,2048]{0,1:T(8,128)(4,1)S(1)} %iota_compare_fusion, bf16[64,128]{1,0:T(8,128)(2,1)} %bitcast.49, bf16[64,2048,1,128]{3,1,2,0:T(8,128)(2,1)} %param.7, bf16[64,128]{1,0:T(8,128)(2,1)} %bitcast.50), kind=kLoop, calls=%fused_computation | loop fusion | flops 33554432 | bytes 134381568 | tf_op jit(solution)/shard_map/jit(_where)/select_n | solution.py:15
  68.5 381.7 %all_to_all.36 = bf16[64,2048,1,128]{3,0,2,1:T(8,128)(2,1)} all-to-all(bf16[64,2048,1,128]{3,0,2,1:T(8,128)(2,1)} %get-tuple-element.18), channel_id=1, replica_groups=mesh['dp'=2,'tp'=4] {'tp'}, dimensions={1} | all-to-all | bytes 67108864 | tf_op jit(solution)/shard_map/all_to_all | solution.py:16
  450.2 9.9 all-to-all-start.1
  460.0 0.0 all-reduce.3.cloned.1.call-start
  460.1 367.2 %all_gather.3 = bf16[64,28,128]{2,0,1:T(8,128)(2,1)S(1)} all-gather(bf16[64,7,128]{2,0,1:T(8,128)(2,1)S(1)} %copy-done), channel_id=1, replica_groups=mesh['dp'=2,'tp'=4] {'tp'}, dimensions={1}, use_global_device_ids=true | all-gather | bytes 573440 | tf_op jit(solution)/shard_map/all_gather | solution.py:18
  827.3 0.1 broadcast_compare_fusion
  827.4 23.4 %copy.33 = bf16[64,2048,1,128]{3,1,0,2:T(8,128)(2,1)} copy(bf16[64,2048,1,128]{3,0,2,1:T(8,128)(2,1)} %all_to_all.36) | data formatting | bytes 67108864 | tf_op jit(solution)/shard_map/all_to_all | solution.py:16
  850.8 16.8 %bitcast_reduce_fusion = (f32[64,4,7]{2,1,0:T(4,128)S(1)}, f32[64,4,512,7]{2,3,1,0:T(8,128)}) fusion(pred[64,512]{1,0:T(8,128)(4,1)S(1)} %broadcast_compare_fusion, bf16[64,512,4,128]{3,1,2,0:T(8,128)(2,1)} %bitcast.40, bf16[64,4,7,128]{3,0,2,1:T(8,128)(2,1)S(1)} %bitcast.44), kind=kOutput, calls=%fused_computation.3 | convolution fusion | flops 237631744 | bytes 37723136 | tf_op jit(solution)/shard_map/bhgd,bthd->bhgt/dot_general | solution.py:22
  867.6 11.6 %pmax.7 = f32[64,4,7]{2,1,0:T(4,128)S(1)} all-reduce(f32[64,4,7]{2,1,0:T(4,128)S(1)} %get-tuple-element.19), channel_id=1, replica_groups=mesh['dp'=2,'tp'=4] {'tp'}, use_global_device_ids=true, to_apply=%region_1.2 | all-reduce | flops 1792 | bytes 14336 | tf_op jit(solution)/shard_map/pmax | solution.py:30
  879.2 3.6 fusion.2
  882.9 23.2 %copy.36 = bf16[64,2048,1,128]{3,1,0,2:T(8,128)(2,1)} copy(bf16[64,2048,1,128]{3,0,2,1:T(8,128)(2,1)} %all-to-all-done.1) | data formatting | bytes 67108864 | tf_op jit(solution)/shard_map/all_to_all | solution.py:17
  906.2 14.5 %fusion.12 = f32[64,4,7,128]{3,2,1,0:T(8,128)S(1)} fusion(bf16[64,512,4,128]{3,1,2,0:T(8,128)(2,1)} %bitcast.41, f32[64,4,512,7]{2,3,1,0:T(8,128)} %get-tuple-element.20, f32[64,4,7]{2,1,0:T(4,128)S(1)} %get-tuple-element.19, pred[64,512]{1,0:T(8,128)(4,1)S(1)} %broadcast_compare_fusion, f32[64,4,7]{2,1,0:T(4,128)S(1)} %bitcast.45), kind=kOutput, calls=%fused_computation.17 | convolution fusion | flops 239697920 | bytes 38189056 | tf_op jit(solution)/shard_map/bhgt,bthd->bhgd/dot_general | solution.py:29
  920.6 0.5 copy.37
  921.2 0.1 reshape.82
  921.3 0.9 copy.39
  922.2 1.4 pad_maximum_fusion
  923.6 0.0 all-reduce.3.cloned.1.call-update
  923.7 0.6 dynamic-slice
  924.9 42.3 %copy.41 = bf16[64,512,4,128]{3,2,1,0:T(4,128)(2,1)} copy(bf16[64,512,4,128]{3,0,1,2:T(8,128)(2,1)} %bitcast.39) | data formatting | bytes 67108864
  967.2 42.3 %copy.42 = bf16[64,512,4,128]{3,2,1,0:T(4,128)(2,1)} copy(bf16[64,512,4,128]{3,0,1,2:T(8,128)(2,1)} %bitcast.17) | data formatting | bytes 67108864
  1009.5 1.1 constant_dynamic-slice_fusion
  1010.6 0.1 copy.47
  1010.7 1.7 fusion.17
  (10 shorter events, 0.1 us)
Async XLA Ops:
  450.2 9.9 copy-start
  450.2 377.2 %copy-start.1 = (s32[64]{0:T(128)S(1)}, s32[64]{0:T(128)}, u32[]{:S(2)}) copy-start(s32[64]{0:T(128)} %param.11) | copy-start | bytes 772
  450.2 432.8 %all-to-all-start.1 = ((bf16[64,2048,1,128]{3,0,2,1:T(8,128)(2,1)}), bf16[64,2048,1,128]{3,0,2,1:T(8,128)(2,1)}, u32[]{:S(2)}, u32[]{:S(2)}) async-start(bf16[64,2048,1,128]{3,0,2,1:T(8,128)(2,1)} %get-tuple-element.17), calls=%async_computation.1 | async-start | bytes 67108864 | tf_op jit(solution)/shard_map/all_to_all | solution.py:17
  460.0 549.5 %all-reduce.3.cloned.1.call-start = ((), (), s32[]{:S(2)}) async-start(), calls=%async_computation.2 | async-start | bytes 3670016
  920.6 3.0 copy-start.2
Sparse Core Ops, SparseCore 0:
  923.8 43.5 all-reduce.2
where the time goes:
time: 1020 us
  blocking collectives  761 us (75%)
  local copies, waits for them, and re-layouts  135 us (13%)
  other arithmetic  68.2 us (7%)
  matrix products  31.2 us (3%)
  between operations  14.8 us (1%)
    all_to_all x1, blocking collectives, local_step(): k_seq = lax.all_to_all(k_upd, 'tp', 1, 2, tiled=True)  382 us
    all_gather x1, blocking collectives, local_step(): q_all = lax.all_gather(query, 'tp', axis=1, tiled=True)  367 us
    unnamed x10, local copies, waits for them, and re-layouts  85.3 us
    select_n x1, other arithmetic, local_step(): v_upd = jnp.where(new_slot, v_new[:, None], v_cache)  60.5 us
    all_to_all x1, local copies, waits for them, and re-layouts, local_step(): k_seq = lax.all_to_all(k_upd, 'tp', 1, 2, tiled=True)  23.4 us
    all_to_all x1, local copies, waits for them, and re-layouts, local_step(): v_seq = lax.all_to_all(v_upd, 'tp', 1, 2, tiled=True)  23.2 us
  transfers between devices with their start and end apart: 2, of which 0 were waited for; matrix products, arithmetic and copies ran while one was open for 13% of the time, Pallas kernels for 0%

commit v1 on v0

v1 whole, which is shorter than its diff:
```python
import functools

import jax
import jax.numpy as jnp
from jax import lax
from jax.experimental import pallas as pl
from jax.experimental.pallas import tpu as pltpu
from jax.sharding import PartitionSpec as P


MASK_VALUE = -1e30

CHUNKS = (1, 3, 6, 8, 8, 8, 8, 8, 6, 4, 2, 1, 1)
PEERS = (2, 3, 1)


def prepare_kernel(first, count, seq_part, me_ref, lens_ref, *refs):
    caches, (new_refs), outs = refs[: 2 * count], refs[2 * count : 2 * count + 2], refs[2 * count + 3 : 3 * count + 3]
    new_rows = refs[3 * count + 3 :]
    req = first + pl.program_id(0)
    rows = lax.broadcasted_iota(jnp.int32, caches[0].shape[1:], 0)
    for t in range(2):
        new_rows[t][...] = new_refs[t][...].astype(jnp.float32)
        row = new_rows[t][pl.ds(req, 1), :]
        for i, x in enumerate(PEERS):
            slot = lens_ref[req] - (me_ref[0] ^ x) * seq_part
            piece = caches[t * count + i][0].astype(jnp.float32)
            outs[i][t, 0] = jnp.where(rows == slot, row, piece).astype(jnp.bfloat16)


def prepare(me, lens, k_cache, v_cache, k_new, v_new, token, first, size, seq_part):
    batch, head_dim = k_new.shape
    count = len(PEERS)
    piece = lambda x: pl.BlockSpec((1, seq_part, head_dim), lambda i, me, lens, x=x: (first + i, me[0] ^ x, 0))
    whole = pl.BlockSpec((batch, head_dim), lambda i, me, lens: (0, 0))
    out = pl.BlockSpec((2, 1, seq_part, head_dim), lambda i, me, lens: (0, i, 0, 0))
    return pl.pallas_call(
        functools.partial(prepare_kernel, first, count, seq_part),
        out_shape=[jax.ShapeDtypeStruct((2, size, seq_part, head_dim), jnp.bfloat16)] * count,
        grid_spec=pltpu.PrefetchScalarGridSpec(
            num_scalar_prefetch=2,
            grid=(size,),
            in_specs=[piece(x) for x in PEERS] * 2 + [whole] * 2 + [pl.BlockSpec(memory_space=pl.ANY)],
            out_specs=[out] * count,
            scratch_shapes=[pltpu.VMEM((batch, head_dim), jnp.float32)] * 2,
        ),
        cost_estimate=pl.CostEstimate(flops=10**6 * size, bytes_accessed=12 * size * seq_part * head_dim * 2, transcendentals=0),
    )(me, lens, *[k_cache] * count, *[v_cache] * count, k_new, v_new, token)


def attention_kernel(lens_ref, q_ref, k_ref, v_ref, k_new_ref, v_new_ref, token_ref, out_ref, k_rows, v_rows):
    req = pl.program_id(0)
    k_rows[...] = k_new_ref[...].astype(jnp.float32)
    v_rows[...] = v_new_ref[...].astype(jnp.float32)
    query = q_ref[0]
    scale = query.shape[-1] ** -0.5
    dims = (((1,), (1,)), ((), ()))
    scores = lax.dot_general(query, k_ref[0], dims, preferred_element_type=jnp.float32) * scale
    positions = lax.broadcasted_iota(jnp.int32, scores.shape, 1)
    valid = positions < lens_ref[req]
    scores = jnp.where(valid, scores, MASK_VALUE)
    new_score = jnp.sum(query.astype(jnp.float32) * k_rows[pl.ds(req, 1), :], axis=-1, keepdims=True) * scale
    top = jnp.maximum(jnp.max(scores, axis=-1, keepdims=True), new_score)
    weights = jnp.where(valid, jnp.exp(scores - top), 0.0)
    new_weight = jnp.exp(new_score - top)
    total = jnp.sum(weights, axis=-1, keepdims=True) + new_weight
    probs = (weights / total).astype(jnp.bfloat16)
    new_prob = (new_weight / total).astype(jnp.bfloat16).astype(jnp.float32)
    out = jnp.dot(probs, v_ref[0], preferred_element_type=jnp.float32) + new_prob * v_rows[pl.ds(req, 1), :]
    out_ref[0] = out.astype(jnp.bfloat16)


def attention(lens, query, k_cache, v_cache, k_new, v_new, token):
    batch, seq_len, head_dim = k_cache.shape
    rows = query.shape[1]
    cache = pl.BlockSpec((1, seq_len, head_dim), lambda i, lens: (i, 0, 0))
    heads = pl.BlockSpec((1, rows, head_dim), lambda i, lens: (i, 0, 0))
    whole = pl.BlockSpec((batch, head_dim), lambda i, lens: (0, 0))
    return pl.pallas_call(
        attention_kernel,
        out_shape=jax.ShapeDtypeStruct(query.shape, jnp.bfloat16),
        grid_spec=pltpu.PrefetchScalarGridSpec(
            num_scalar_prefetch=1,
            grid=(batch,),
            in_specs=[heads, cache, cache, whole, whole, pl.BlockSpec(memory_space=pl.ANY)],
            out_specs=heads,
            scratch_shapes=[pltpu.VMEM((batch, head_dim), jnp.float32)] * 2,
        ),
        cost_estimate=pl.CostEstimate(flops=10**8, bytes_accessed=k_cache.size * 4, transcendentals=0),
        name="attention",
    )(lens, query, k_cache, v_cache, k_new, v_new, token)


def interleave_kernel(first, seq_part, n_skip, me_ref, lens_ref, *refs):
    count = len(PEERS)
    owns, pieces, new_refs = refs[:2], refs[2 : 2 + count], refs[2 + count : 4 + count]
    outs, (mixed, *new_rows) = refs[4 + count + n_skip : 6 + count + n_skip], refs[6 + count + n_skip :]
    req = first + pl.program_id(0)
    me = me_ref[0]
    heads = count + 1
    rows = lax.broadcasted_iota(jnp.int32, owns[0].shape[1:], 0)
    slot = lens_ref[req] - me * seq_part
    for t in range(2):
        new_rows[t][...] = new_refs[t][...].astype(jnp.float32)
        row = new_rows[t][pl.ds(req, 1), :]
        mixed[pl.ds(me, seq_part, heads), :] = jnp.where(rows == slot, row, owns[t][0].astype(jnp.float32))
        for i, x in enumerate(PEERS):
            mixed[pl.ds(me ^ x, seq_part, heads), :] = pieces[i][t, 0].astype(jnp.float32)
        outs[t][0] = mixed[...].astype(jnp.bfloat16)


def interleave(me, lens, k_cache, v_cache, pieces, k_new, v_new, bufs, tokens, first, size, seq_part):
    batch, head_dim = k_new.shape
    heads = len(PEERS) + 1
    own = pl.BlockSpec((1, seq_part, head_dim), lambda i, me, lens: (first + i, me[0], 0))
    piece = pl.BlockSpec((2, 1, seq_part, head_dim), lambda i, me, lens: (0, i, 0, 0))
    whole = pl.BlockSpec((batch, head_dim), lambda i, me, lens: (0, 0))
    out = pl.BlockSpec((1, seq_part * heads, head_dim), lambda i, me, lens: (first + i, 0, 0))
    skipped = list(bufs) + list(tokens)
    n_lead = 2 + 2 + len(pieces) + 2
    return pl.pallas_call(
        functools.partial(interleave_kernel, first, seq_part, len(skipped)),
        out_shape=[jax.ShapeDtypeStruct((batch, seq_part * heads, head_dim), jnp.bfloat16)] * 2,
        grid_spec=pltpu.PrefetchScalarGridSpec(
            num_scalar_prefetch=2,
            grid=(size,),
            in_specs=[own] * 2 + [piece] * len(pieces) + [whole] * 2 + [pl.BlockSpec(memory_space=pl.ANY)] * len(skipped),
            out_specs=[out] * 2,
            scratch_shapes=[pltpu.VMEM((seq_part * heads, head_dim), jnp.float32)] + [pltpu.VMEM((batch, head_dim), jnp.float32)] * 2,
        ),
        input_output_aliases={n_lead + i: i for i in range(len(bufs))},
        cost_estimate=pl.CostEstimate(flops=10**6 * size, bytes_accessed=16 * size * seq_part * head_dim * 2, transcendentals=0),
    )(me, lens, k_cache, v_cache, *pieces, k_new, v_new, *skipped)


def solution(mesh):
    n_tp = mesh.shape["tp"]

    def local_step(query, k_cache, v_cache, k_new, v_new, lens):
        batch, seq_len, _, head_dim = k_cache.shape
        seq_part = seq_len // n_tp
        group = query.shape[1]
        me = lax.axis_index("tp").astype(jnp.int32).reshape(1)
        k_cache, v_cache = k_cache.reshape(batch, seq_len, head_dim), v_cache.reshape(batch, seq_len, head_dim)
        k_new, v_new = k_new.reshape(batch, head_dim), v_new.reshape(batch, head_dim)

        token, arrived, first = lens, [], 0
        for size in CHUNKS:
            sends = prepare(me, lens, k_cache, v_cache, k_new, v_new, token, first, size, seq_part)
            pieces = []
            for s, x in zip(sends, PEERS):
                pieces.append(lax.ppermute(s, "tp", [(i, i ^ x) for i in range(n_tp)]))
            arrived.append(pieces)
            token, first = sends[0], first + size

        rows = jnp.pad(query, ((0, 0), (0, 8 - group), (0, 0)))
        attn_out = attention(lens, rows, k_cache, v_cache, k_new, v_new, token)

        bufs, tokens, first = (), (attn_out,), 0
        for size, pieces in zip(CHUNKS, arrived):
            bufs = interleave(me, lens, k_cache, v_cache, pieces, k_new, v_new, bufs, tokens, first, size, seq_part)
            tokens, first = (), first + size
        k_seq, v_seq = (b.reshape(batch, seq_part, n_tp, head_dim) for b in bufs)
        return attn_out[:, :group], k_seq, v_seq

    head_spec = P("dp", "tp")
    entry_spec = P("dp", None, "tp")
    return jax.shard_map(local_step, mesh=mesh, in_specs=(head_spec, entry_spec, entry_spec, head_spec, head_spec, P("dp")), out_specs=(head_spec, P("dp", "tp"), P("dp", "tp")), check_vma=False)
```

time: 1020 us -> 955 us (0.936)
  blocking collectives: 761 us -> 0 us
  waiting for transfers between devices: 0.02 us -> 662 us
  Pallas kernels: 0 us -> 247 us
  local copies, waits for them, and re-layouts: 135 us -> 10.2 us
  other arithmetic: 68.2 us -> 0 us
  matrix products: 31.2 us -> 0 us
  starting transfers between devices: 9.89 us -> 31.8 us
  between operations: 14.8 us -> 0.84 us
    ppermute x0 -> x39, waiting for transfers between devices: none -> 662 us  [local_step(): pieces.append(lax.ppermute(s, 'tp', [(i, i ^ x) for i in range(n_tp)]))]
    all_to_all x1 -> x0, blocking collectives: 382 us -> none  [local_step(): k_seq = lax.all_to_all(k_upd, 'tp', 1, 2, tiled=True)]
    all_gather x1 -> x0, blocking collectives: 367 us -> none  [local_step(): q_all = lax.all_gather(query, 'tp', axis=1, tiled=True)]
    pallas_call x0 -> x27, Pallas kernels: none -> 247 us  [the longest x13 93.2 us: interleave(): pl.pallas_call(functools.partial(interleave_kernel, first, seq_part, len(...]
    unnamed x10 -> x56, local copies, waits for them, and re-layouts: 85.3 us -> 9.55 us
    select_n x1 -> x0, other arithmetic: 60.5 us -> none  [local_step(): v_upd = jnp.where(new_slot, v_new[:, None], v_cache)]
    all_to_all x2 -> x0, local copies, waits for them, and re-layouts: 46.6 us -> none  [the longest x1 23.4 us: local_step(): k_seq = lax.all_to_all(k_upd, 'tp', 1, 2, tiled=True)]
    ppermute x0 -> x39, starting transfers between devices: none -> 31.8 us  [local_step(): pieces.append(lax.ppermute(s, 'tp', [(i, i ^ x) for i in range(n_tp)]))]
  transfers between devices with their start and end apart: 2 -> 39, of which waited for: 0 -> 17; matrix products, arithmetic and copies ran while one was open for 13% -> 0% of each run, Pallas kernels for 0% -> 25%
where the time goes in v1:
time: 955 us; the launch traced here: 951 us
  waiting for transfers between devices  662 us (69%)
  Pallas kernels  247 us (26%)
  starting transfers between devices  31.8 us (3%)
  local copies, waits for them, and re-layouts  10.2 us (1%)
    ppermute x39, waiting for transfers between devices, local_step(): pieces.append(lax.ppermute(s, 'tp', [(i, i ^ x) for i in range(n_tp)]))  662 us
    pallas_call x13, Pallas kernels, interleave(): pl.pallas_call(functools.partial(interleave_kernel, first, seq_part, len(...  93.2 us
    pallas_call x13, Pallas kernels, prepare(): pl.pallas_call(functools.partial(prepare_kernel, first, count, seq_part),...  90.5 us
    pallas_call x1, Pallas kernels, attention(): pl.pallas_call(attention_kernel, out_shape=jax.ShapeDtypeStruct(query.sha...  62.8 us
    ppermute x39, starting transfers between devices, local_step(): pieces.append(lax.ppermute(s, 'tp', [(i, i ^ x) for i in range(n_tp)]))  31.8 us
  transfers between devices with their start and end apart: 39, of which 17 were waited for; matrix products, arithmetic and copies ran while one was open for 0% of the time, Pallas kernels for 25%

profile of v1, /device:TPU:0, one launch (start us, length us, event | category | flops | bytes accessed | tf_op | source)
XLA Modules:
  0.0 951.0 jit_solution(11708229947631300239)
XLA Ops:
  29.7 10.1 %shard_map.89 = (bf16[2,8,512,128]{3,2,1,0:T(8,128)(2,1)}, bf16[2,8,512,128]{3,2,1,0:T(8,128)(2,1)}, bf16[2,8,512,128]{3,2,1,0:T(8,128)(2,1)}) custom-call(s32[1]{0:T(128)} %bitcast.4.me_ref, s32[64]{0:T(128)} %lens_ref.53, bf16[64,2048,128]{2,1,0:T(8,128)(2,1)} %bitcast.20, bf16[64,2048,128]{2,1,0:T(8,128)(2,1)} %bitcast.21, ...), custom_call_target="tpu_custom_call" | custom-call | flops 8000000 | bytes 12582912 | tf_op jit(solution)/shard_map/pallas_call | solution.py:37
  49.9 10.1 %shard_map.91 = (bf16[2,8,512,128]{3,2,1,0:T(8,128)(2,1)}, bf16[2,8,512,128]{3,2,1,0:T(8,128)(2,1)}, bf16[2,8,512,128]{3,2,1,0:T(8,128)(2,1)}) custom-call(s32[1]{0:T(128)} %bitcast.4.me_ref, s32[64]{0:T(128)} %lens_ref.53, bf16[64,2048,128]{2,1,0:T(8,128)(2,1)} %bitcast.26, bf16[64,2048,128]{2,1,0:T(8,128)(2,1)} %bitcast.27, ...), custom_call_target="tpu_custom_call" | custom-call | flops 8000000 | bytes 12582912 | tf_op jit(solution)/shard_map/pallas_call | solution.py:37
  95.1 13.5 %collective-permute-done.36.refs_2_ = bf16[2,1,512,128]{3,2,1,0:T(8,128)(2,1)} collective-permute-done((bf16[2,1,512,128]{3,2,1,0:T(8,128)(2,1)}, bf16[2,1,512,128]{3,2,1,0:T(8,128)(2,1)}, u32[]{:S(2)}, u32[]{:S(2)}) %collective-permute-start.36) | collective-permute-done | bytes 262176 | tf_op jit(solution)/shard_map/ppermute | solution.py:152
  115.6 26.6 %collective-permute-done.6.refs_2_ = bf16[2,2,512,128]{3,2,1,0:T(8,128)(2,1)S(1)} collective-permute-done((bf16[2,2,512,128]{3,2,1,0:T(8,128)(2,1)}, bf16[2,2,512,128]{3,2,1,0:T(8,128)(2,1)S(1)}, u32[]{:S(2)}, u32[]{:S(2)}) %collective-permute-start.6) | collective-permute-done | bytes 524320 | tf_op jit(solution)/shard_map/ppermute | solution.py:152
  144.3 92.5 %collective-permute-done.33.refs_2_ = bf16[2,3,512,128]{3,2,1,0:T(8,128)(2,1)S(1)} collective-permute-done((bf16[2,3,512,128]{3,2,1,0:T(8,128)(2,1)}, bf16[2,3,512,128]{3,2,1,0:T(8,128)(2,1)S(1)}, u32[]{:S(2)}, u32[]{:S(2)}) %collective-permute-start.33) | collective-permute-done | bytes 786464 | tf_op jit(solution)/shard_map/ppermute | solution.py:152
  243.4 31.8 %collective-permute-done.30.refs_2_ = bf16[2,6,512,128]{3,2,1,0:T(8,128)(2,1)S(1)} collective-permute-done((bf16[2,6,512,128]{3,2,1,0:T(8,128)(2,1)}, bf16[2,6,512,128]{3,2,1,0:T(8,128)(2,1)S(1)}, u32[]{:S(2)}, u32[]{:S(2)}) %collective-permute-start.30) | collective-permute-done | bytes 1572896 | tf_op jit(solution)/shard_map/ppermute | solution.py:152
  276.4 30.7 %collective-permute-done.13.refs_3_ = bf16[2,6,512,128]{3,2,1,0:T(8,128)(2,1)} collective-permute-done((bf16[2,6,512,128]{3,2,1,0:T(8,128)(2,1)}, bf16[2,6,512,128]{3,2,1,0:T(8,128)(2,1)}, u32[]{:S(2)}, u32[]{:S(2)}) %collective-permute-start.13) | collective-permute-done | bytes 1572896 | tf_op jit(solution)/shard_map/ppermute | solution.py:152
  311.4 31.2 %collective-permute-done.12.refs_2_ = bf16[2,6,512,128]{3,2,1,0:T(8,128)(2,1)S(1)} collective-permute-done((bf16[2,6,512,128]{3,2,1,0:T(8,128)(2,1)}, bf16[2,6,512,128]{3,2,1,0:T(8,128)(2,1)S(1)}, u32[]{:S(2)}, u32[]{:S(2)}) %collective-permute-start.12) | collective-permute-done | bytes 1572896 | tf_op jit(solution)/shard_map/ppermute | solution.py:152
  343.8 42.0 %collective-permute-done.28.refs_3_ = bf16[2,8,512,128]{3,2,1,0:T(8,128)(2,1)S(1)} collective-permute-done((bf16[2,8,512,128]{3,2,1,0:T(8,128)(2,1)}, bf16[2,8,512,128]{3,2,1,0:T(8,128)(2,1)S(1)}, u32[]{:S(2)}, u32[]{:S(2)}) %collective-permute-start.28) | collective-permute-done | bytes 2097184 | tf_op jit(solution)/shard_map/ppermute | solution.py:152
  388.7 43.8 %collective-permute-done.27.refs_2_ = bf16[2,8,512,128]{3,2,1,0:T(8,128)(2,1)S(1)} collective-permute-done((bf16[2,8,512,128]{3,2,1,0:T(8,128)(2,1)}, bf16[2,8,512,128]{3,2,1,0:T(8,128)(2,1)S(1)}, u32[]{:S(2)}, u32[]{:S(2)}) %collective-permute-start.27) | collective-permute-done | bytes 2097184 | tf_op jit(solution)/shard_map/ppermute | solution.py:152
  432.5 43.1 %collective-permute-done.25.refs_3_ = bf16[2,8,512,128]{3,2,1,0:T(8,128)(2,1)S(1)} collective-permute-done((bf16[2,8,512,128]{3,2,1,0:T(8,128)(2,1)}, bf16[2,8,512,128]{3,2,1,0:T(8,128)(2,1)S(1)}, u32[]{:S(2)}, u32[]{:S(2)}) %collective-permute-start.25) | collective-permute-done | bytes 2097184 | tf_op jit(solution)/shard_map/ppermute | solution.py:152
  478.6 43.8 %collective-permute-done.24.refs_2_ = bf16[2,8,512,128]{3,2,1,0:T(8,128)(2,1)S(1)} collective-permute-done((bf16[2,8,512,128]{3,2,1,0:T(8,128)(2,1)}, bf16[2,8,512,128]{3,2,1,0:T(8,128)(2,1)S(1)}, u32[]{:S(2)}, u32[]{:S(2)}) %collective-permute-start.24) | collective-permute-done | bytes 2097184 | tf_op jit(solution)/shard_map/ppermute | solution.py:152
  522.4 43.1 %collective-permute-done.22.refs_3_ = bf16[2,8,512,128]{3,2,1,0:T(8,128)(2,1)S(1)} collective-permute-done((bf16[2,8,512,128]{3,2,1,0:T(8,128)(2,1)}, bf16[2,8,512,128]{3,2,1,0:T(8,128)(2,1)S(1)}, u32[]{:S(2)}, u32[]{:S(2)}) %collective-permute-start.22) | collective-permute-done | bytes 2097184 | tf_op jit(solution)/shard_map/ppermute | solution.py:152
  568.5 43.8 %collective-permute-done.21.refs_2_ = bf16[2,8,512,128]{3,2,1,0:T(8,128)(2,1)S(1)} collective-permute-done((bf16[2,8,512,128]{3,2,1,0:T(8,128)(2,1)}, bf16[2,8,512,128]{3,2,1,0:T(8,128)(2,1)S(1)}, u32[]{:S(2)}, u32[]{:S(2)}) %collective-permute-start.21) | collective-permute-done | bytes 2097184 | tf_op jit(solution)/shard_map/ppermute | solution.py:152
  612.3 43.1 %collective-permute-done.19.refs_3_ = bf16[2,8,512,128]{3,2,1,0:T(8,128)(2,1)S(1)} collective-permute-done((bf16[2,8,512,128]{3,2,1,0:T(8,128)(2,1)}, bf16[2,8,512,128]{3,2,1,0:T(8,128)(2,1)S(1)}, u32[]{:S(2)}, u32[]{:S(2)}) %collective-permute-start.19) | collective-permute-done | bytes 2097184 | tf_op jit(solution)/shard_map/ppermute | solution.py:152
  661.3 40.9 %collective-permute-done.18.refs_2_ = bf16[2,8,512,128]{3,2,1,0:T(8,128)(2,1)} collective-permute-done((bf16[2,8,512,128]{3,2,1,0:T(8,128)(2,1)}, bf16[2,8,512,128]{3,2,1,0:T(8,128)(2,1)}, u32[]{:S(2)}, u32[]{:S(2)}) %collective-permute-start.18) | collective-permute-done | bytes 2097184 | tf_op jit(solution)/shard_map/ppermute | solution.py:152
  702.2 43.0 %collective-permute-done.16.refs_3_ = bf16[2,8,512,128]{3,2,1,0:T(8,128)(2,1)} collective-permute-done((bf16[2,8,512,128]{3,2,1,0:T(8,128)(2,1)}, bf16[2,8,512,128]{3,2,1,0:T(8,128)(2,1)}, u32[]{:S(2)}, u32[]{:S(2)}) %collective-permute-start.16) | collective-permute-done | bytes 2097184 | tf_op jit(solution)/shard_map/ppermute | solution.py:152
  747.2 44.9 %collective-permute-done.15.refs_2_ = bf16[2,8,512,128]{3,2,1,0:T(8,128)(2,1)} collective-permute-done((bf16[2,8,512,128]{3,2,1,0:T(8,128)(2,1)S(1)}, bf16[2,8,512,128]{3,2,1,0:T(8,128)(2,1)}, u32[]{:S(2)}, u32[]{:S(2)}) %collective-permute-start.15) | collective-permute-done | bytes 2097184 | tf_op jit(solution)/shard_map/ppermute | solution.py:152
  793.5 62.8 %attention.1.refs_7_ = bf16[64,8,128]{2,1,0:T(8,128)(2,1)} custom-call(s32[64]{0:T(128)} %lens_ref.53, bf16[64,8,128]{2,1,0:T(8,128)(2,1)} %pad.4.q_ref, bf16[64,2048,128]{2,1,0:T(8,128)(2,1)} %bitcast.47, bf16[64,2048,128]{2,1,0:T(8,128)(2,1)} %bitcast.100, bf16[64,128]{1,0:T(8,128)(2,1)} %bitcast.129, bf16[64,128]{1,0:T(8,128)(2,1)} %bitcast.156, ...), custom_call_target="tpu_custom_call" | custom-call | flops 100000000 | bytes 67108864 | tf_op jit(solution)/shard_map/attention/pallas_call | solution.py:79
  874.6 10.5 %shard_map.101 = (bf16[64,2048,128]{2,1,0:T(8,128)(2,1)}, bf16[64,2048,128]{2,1,0:T(8,128)(2,1)}) custom-call(s32[1]{0:T(128)} %bitcast.4.me_ref, s32[64]{0:T(128)} %lens_ref.53, bf16[64,2048,128]{2,1,0:T(8,128)(2,1)} %bitcast.51, bf16[64,2048,128]{2,1,0:T(8,128)(2,1)} %bitcast.104, ...), custom_call_target="tpu_custom_call", output_to_operand_aliasing={{0}: (9, {}), {1}: (10, {})} | custom-call | flops 8000000 | bytes 16777216 | tf_op jit(solution)/shard_map/pallas_call | solution.py:121
  885.0 10.5 %shard_map.102 = (bf16[64,2048,128]{2,1,0:T(8,128)(2,1)}, bf16[64,2048,128]{2,1,0:T(8,128)(2,1)}) custom-call(s32[1]{0:T(128)} %bitcast.4.me_ref, s32[64]{0:T(128)} %lens_ref.53, bf16[64,2048,128]{2,1,0:T(8,128)(2,1)} %bitcast.52, bf16[64,2048,128]{2,1,0:T(8,128)(2,1)} %bitcast.105, ...), custom_call_target="tpu_custom_call", output_to_operand_aliasing={{0}: (9, {}), {1}: (10, {})} | custom-call | flops 8000000 | bytes 16777216 | tf_op jit(solution)/shard_map/pallas_call | solution.py:121
  895.5 10.5 %shard_map.103 = (bf16[64,2048,128]{2,1,0:T(8,128)(2,1)}, bf16[64,2048,128]{2,1,0:T(8,128)(2,1)}) custom-call(s32[1]{0:T(128)} %bitcast.4.me_ref, s32[64]{0:T(128)} %lens_ref.53, bf16[64,2048,128]{2,1,0:T(8,128)(2,1)} %bitcast.53, bf16[64,2048,128]{2,1,0:T(8,128)(2,1)} %bitcast.106, ...), custom_call_target="tpu_custom_call", output_to_operand_aliasing={{0}: (9, {}), {1}: (10, {})} | custom-call | flops 8000000 | bytes 16777216 | tf_op jit(solution)/shard_map/pallas_call | solution.py:121
  906.0 10.5 %shard_map.104 = (bf16[64,2048,128]{2,1,0:T(8,128)(2,1)}, bf16[64,2048,128]{2,1,0:T(8,128)(2,1)}) custom-call(s32[1]{0:T(128)} %bitcast.4.me_ref, s32[64]{0:T(128)} %lens_ref.53, bf16[64,2048,128]{2,1,0:T(8,128)(2,1)} %bitcast.54, bf16[64,2048,128]{2,1,0:T(8,128)(2,1)} %bitcast.107, ...), custom_call_target="tpu_custom_call", output_to_operand_aliasing={{0}: (9, {}), {1}: (10, {})} | custom-call | flops 8000000 | bytes 16777216 | tf_op jit(solution)/shard_map/pallas_call | solution.py:121
  916.4 10.5 %shard_map.105 = (bf16[64,2048,128]{2,1,0:T(8,128)(2,1)}, bf16[64,2048,128]{2,1,0:T(8,128)(2,1)}) custom-call(s32[1]{0:T(128)} %bitcast.4.me_ref, s32[64]{0:T(128)} %lens_ref.53, bf16[64,2048,128]{2,1,0:T(8,128)(2,1)} %bitcast.55, bf16[64,2048,128]{2,1,0:T(8,128)(2,1)} %bitcast.108, ...), custom_call_target="tpu_custom_call", output_to_operand_aliasing={{0}: (9, {}), {1}: (10, {})} | custom-call | flops 8000000 | bytes 16777216 | tf_op jit(solution)/shard_map/pallas_call | solution.py:121
  (138 shorter events, 157.1 us)
Async XLA Ops:
  113.8 127.1 %collective-permute-start.31 = (bf16[2,6,512,128]{3,2,1,0:T(8,128)(2,1)}, bf16[2,6,512,128]{3,2,1,0:T(8,128)(2,1)S(1)}, u32[]{:S(2)}, u32[]{:S(2)}) collective-permute-start(bf16[2,6,512,128]{3,2,1,0:T(8,128)(2,1)} %get-tuple-element.101), channel_id=1, source_target_pairs={{0,3},{1,2},{2,1},{3,0},{4,7},{5,6},{6,5},{7,4}} | collective-permute-start | bytes 4718600 | tf_op jit(solution)/shard_map/ppermute | solution.py:152
  115.6 122.1 %collective-permute-start.10 = (bf16[2,4,512,128]{3,2,1,0:T(8,128)(2,1)}, bf16[2,4,512,128]{3,2,1,0:T(8,128)(2,1)}, u32[]{:S(2)}, u32[]{:S(2)}) collective-permute-start(bf16[2,4,512,128]{3,2,1,0:T(8,128)(2,1)} %get-tuple-element.87), channel_id=1, source_target_pairs={{0,3},{1,2},{2,1},{3,0},{4,7},{5,6},{6,5},{7,4}} | collective-permute-start | bytes 3145736 | tf_op jit(solution)/shard_map/ppermute | solution.py:152
  142.2 96.5 %collective-permute-start.9 = (bf16[2,4,512,128]{3,2,1,0:T(8,128)(2,1)S(1)}, bf16[2,4,512,128]{3,2,1,0:T(8,128)(2,1)S(1)}, u32[]{:S(2)}, u32[]{:S(2)}) collective-permute-start(bf16[2,4,512,128]{3,2,1,0:T(8,128)(2,1)S(1)} %copy-done.18), channel_id=1, source_target_pairs={{0,2},{1,3},{2,0},{3,1},{4,6},{5,7},{6,4},{7,5}} | collective-permute-start | bytes 3145736 | tf_op jit(solution)/shard_map/ppermute | solution.py:152
  240.9 101.7 %collective-permute-start.12 = (bf16[2,6,512,128]{3,2,1,0:T(8,128)(2,1)}, bf16[2,6,512,128]{3,2,1,0:T(8,128)(2,1)S(1)}, u32[]{:S(2)}, u32[]{:S(2)}) collective-permute-start(bf16[2,6,512,128]{3,2,1,0:T(8,128)(2,1)} %get-tuple-element.76.refs_8_), channel_id=1, source_target_pairs={{0,2},{1,3},{2,0},{3,1},{4,6},{5,7},{6,4},{7,5}} | collective-permute-start | bytes 4718600 | tf_op jit(solution)/shard_map/ppermute | solution.py:152
  243.2 142.5 %collective-permute-start.28 = (bf16[2,8,512,128]{3,2,1,0:T(8,128)(2,1)}, bf16[2,8,512,128]{3,2,1,0:T(8,128)(2,1)S(1)}, u32[]{:S(2)}, u32[]{:S(2)}) collective-permute-start(bf16[2,8,512,128]{3,2,1,0:T(8,128)(2,1)} %get-tuple-element.99), channel_id=1, source_target_pairs={{0,3},{1,2},{2,1},{3,0},{4,7},{5,6},{6,5},{7,4}} | collective-permute-start | bytes 6291464 | tf_op jit(solution)/shard_map/ppermute | solution.py:152
  276.4 110.8 %collective-permute-start.29 = (bf16[2,8,512,128]{3,2,1,0:T(8,128)(2,1)}, bf16[2,8,512,128]{3,2,1,0:T(8,128)(2,1)S(1)}, u32[]{:S(2)}, u32[]{:S(2)}) collective-permute-start(bf16[2,8,512,128]{3,2,1,0:T(8,128)(2,1)} %get-tuple-element.100), channel_id=1, source_target_pairs={{0,1},{1,0},{2,3},{3,2},{4,5},{5,4},{6,7},{7,6}} | collective-permute-start | bytes 6291464 | tf_op jit(solution)/shard_map/ppermute | solution.py:152
  307.1 125.4 %collective-permute-start.27 = (bf16[2,8,512,128]{3,2,1,0:T(8,128)(2,1)}, bf16[2,8,512,128]{3,2,1,0:T(8,128)(2,1)S(1)}, u32[]{:S(2)}, u32[]{:S(2)}) collective-permute-start(bf16[2,8,512,128]{3,2,1,0:T(8,128)(2,1)} %get-tuple-element.71.refs_8_), channel_id=1, source_target_pairs={{0,2},{1,3},{2,0},{3,1},{4,6},{5,7},{6,4},{7,5}} | collective-permute-start | bytes 6291464 | tf_op jit(solution)/shard_map/ppermute | solution.py:152
  309.8 165.9 %collective-permute-start.25 = (bf16[2,8,512,128]{3,2,1,0:T(8,128)(2,1)}, bf16[2,8,512,128]{3,2,1,0:T(8,128)(2,1)S(1)}, u32[]{:S(2)}, u32[]{:S(2)}) collective-permute-start(bf16[2,8,512,128]{3,2,1,0:T(8,128)(2,1)} %get-tuple-element.97), channel_id=1, source_target_pairs={{0,3},{1,2},{2,1},{3,0},{4,7},{5,6},{6,5},{7,4}} | collective-permute-start | bytes 6291464 | tf_op jit(solution)/shard_map/ppermute | solution.py:152
  343.8 133.3 %collective-permute-start.26 = (bf16[2,8,512,128]{3,2,1,0:T(8,128)(2,1)}, bf16[2,8,512,128]{3,2,1,0:T(8,128)(2,1)S(1)}, u32[]{:S(2)}, u32[]{:S(2)}) collective-permute-start(bf16[2,8,512,128]{3,2,1,0:T(8,128)(2,1)} %get-tuple-element.98), channel_id=1, source_target_pairs={{0,1},{1,0},{2,3},{3,2},{4,5},{5,4},{6,7},{7,6}} | collective-permute-start | bytes 6291464 | tf_op jit(solution)/shard_map/ppermute | solution.py:152
  385.7 136.6 %collective-permute-start.24 = (bf16[2,8,512,128]{3,2,1,0:T(8,128)(2,1)}, bf16[2,8,512,128]{3,2,1,0:T(8,128)(2,1)S(1)}, u32[]{:S(2)}, u32[]{:S(2)}) collective-permute-start(bf16[2,8,512,128]{3,2,1,0:T(8,128)(2,1)} %get-tuple-element.72.refs_8_), channel_id=1, source_target_pairs={{0,2},{1,3},{2,0},{3,1},{4,6},{5,7},{6,4},{7,5}} | collective-permute-start | bytes 6291464 | tf_op jit(solution)/shard_map/ppermute | solution.py:152
  387.2 178.3 %collective-permute-start.22 = (bf16[2,8,512,128]{3,2,1,0:T(8,128)(2,1)}, bf16[2,8,512,128]{3,2,1,0:T(8,128)(2,1)S(1)}, u32[]{:S(2)}, u32[]{:S(2)}) collective-permute-start(bf16[2,8,512,128]{3,2,1,0:T(8,128)(2,1)} %get-tuple-element.95), channel_id=1, source_target_pairs={{0,3},{1,2},{2,1},{3,0},{4,7},{5,6},{6,5},{7,4}} | collective-permute-start | bytes 6291464 | tf_op jit(solution)/shard_map/ppermute | solution.py:152
  432.5 134.5 %collective-permute-start.23 = (bf16[2,8,512,128]{3,2,1,0:T(8,128)(2,1)}, bf16[2,8,512,128]{3,2,1,0:T(8,128)(2,1)S(1)}, u32[]{:S(2)}, u32[]{:S(2)}) collective-permute-start(bf16[2,8,512,128]{3,2,1,0:T(8,128)(2,1)} %get-tuple-element.96), channel_id=1, source_target_pairs={{0,1},{1,0},{2,3},{3,2},{4,5},{5,4},{6,7},{7,6}} | collective-permute-start | bytes 6291464 | tf_op jit(solution)/shard_map/ppermute | solution.py:152
  475.6 136.6 %collective-permute-start.21 = (bf16[2,8,512,128]{3,2,1,0:T(8,128)(2,1)}, bf16[2,8,512,128]{3,2,1,0:T(8,128)(2,1)S(1)}, u32[]{:S(2)}, u32[]{:S(2)}) collective-permute-start(bf16[2,8,512,128]{3,2,1,0:T(8,128)(2,1)} %get-tuple-element.73.refs_8_), channel_id=1, source_target_pairs={{0,2},{1,3},{2,0},{3,1},{4,6},{5,7},{6,4},{7,5}} | collective-permute-start | bytes 6291464 | tf_op jit(solution)/shard_map/ppermute | solution.py:152
  477.1 178.3 %collective-permute-start.19 = (bf16[2,8,512,128]{3,2,1,0:T(8,128)(2,1)}, bf16[2,8,512,128]{3,2,1,0:T(8,128)(2,1)S(1)}, u32[]{:S(2)}, u32[]{:S(2)}) collective-permute-start(bf16[2,8,512,128]{3,2,1,0:T(8,128)(2,1)} %get-tuple-element.93), channel_id=1, source_target_pairs={{0,3},{1,2},{2,1},{3,0},{4,7},{5,6},{6,5},{7,4}} | collective-permute-start | bytes 6291464 | tf_op jit(solution)/shard_map/ppermute | solution.py:152
  522.4 137.7 %collective-permute-start.20 = (bf16[2,8,512,128]{3,2,1,0:T(8,128)(2,1)}, bf16[2,8,512,128]{3,2,1,0:T(8,128)(2,1)}, u32[]{:S(2)}, u32[]{:S(2)}) collective-permute-start(bf16[2,8,512,128]{3,2,1,0:T(8,128)(2,1)} %get-tuple-element.94), channel_id=1, source_target_pairs={{0,1},{1,0},{2,3},{3,2},{4,5},{5,4},{6,7},{7,6}} | collective-permute-start | bytes 6291464 | tf_op jit(solution)/shard_map/ppermute | solution.py:152
  565.5 136.7 %collective-permute-start.18 = (bf16[2,8,512,128]{3,2,1,0:T(8,128)(2,1)}, bf16[2,8,512,128]{3,2,1,0:T(8,128)(2,1)}, u32[]{:S(2)}, u32[]{:S(2)}) collective-permute-start(bf16[2,8,512,128]{3,2,1,0:T(8,128)(2,1)} %get-tuple-element.74.refs_8_), channel_id=1, source_target_pairs={{0,2},{1,3},{2,0},{3,1},{4,6},{5,7},{6,4},{7,5}} | collective-permute-start | bytes 6291464 | tf_op jit(solution)/shard_map/ppermute | solution.py:152
  567.0 178.3 %collective-permute-start.16 = (bf16[2,8,512,128]{3,2,1,0:T(8,128)(2,1)}, bf16[2,8,512,128]{3,2,1,0:T(8,128)(2,1)}, u32[]{:S(2)}, u32[]{:S(2)}) collective-permute-start(bf16[2,8,512,128]{3,2,1,0:T(8,128)(2,1)} %get-tuple-element.91), channel_id=1, source_target_pairs={{0,3},{1,2},{2,1},{3,0},{4,7},{5,6},{6,5},{7,4}} | collective-permute-start | bytes 6291464 | tf_op jit(solution)/shard_map/ppermute | solution.py:152
  612.3 134.9 %collective-permute-start.17 = (bf16[2,8,512,128]{3,2,1,0:T(8,128)(2,1)}, bf16[2,8,512,128]{3,2,1,0:T(8,128)(2,1)}, u32[]{:S(2)}, u32[]{:S(2)}) collective-permute-start(bf16[2,8,512,128]{3,2,1,0:T(8,128)(2,1)} %get-tuple-element.92), channel_id=1, source_target_pairs={{0,1},{1,0},{2,3},{3,2},{4,5},{5,4},{6,7},{7,6}} | collective-permute-start | bytes 6291464 | tf_op jit(solution)/shard_map/ppermute | solution.py:152
  655.4 136.7 %collective-permute-start.15 = (bf16[2,8,512,128]{3,2,1,0:T(8,128)(2,1)S(1)}, bf16[2,8,512,128]{3,2,1,0:T(8,128)(2,1)}, u32[]{:S(2)}, u32[]{:S(2)}) collective-permute-start(bf16[2,8,512,128]{3,2,1,0:T(8,128)(2,1)S(1)} %copy-done), channel_id=1, source_target_pairs={{0,2},{1,3},{2,0},{3,1},{4,6},{5,7},{6,4},{7,5}} | collective-permute-start | bytes 6291464 | tf_op jit(solution)/shard_map/ppermute | solution.py:152
  660.1 284.6 %collective-permute-start.3 = (bf16[2,1,512,128]{3,2,1,0:T(8,128)(2,1)}, bf16[2,1,512,128]{3,2,1,0:T(8,128)(2,1)}, u32[]{:S(2)}, u32[]{:S(2)}) collective-permute-start(bf16[2,1,512,128]{3,2,1,0:T(8,128)(2,1)} %get-tuple-element.79.refs_8_), channel_id=1, source_target_pairs={{0,2},{1,3},{2,0},{3,1},{4,6},{5,7},{6,4},{7,5}} | collective-permute-start | bytes 786440 | tf_op jit(solution)/shard_map/ppermute | solution.py:152
  702.2 242.4 %collective-permute-start.5 = (bf16[2,1,512,128]{3,2,1,0:T(8,128)(2,1)}, bf16[2,1,512,128]{3,2,1,0:T(8,128)(2,1)}, u32[]{:S(2)}, u32[]{:S(2)}) collective-permute-start(bf16[2,1,512,128]{3,2,1,0:T(8,128)(2,1)} %get-tuple-element.84), channel_id=1, source_target_pairs={{0,1},{1,0},{2,3},{3,2},{4,5},{5,4},{6,7},{7,6}} | collective-permute-start | bytes 786440 | tf_op jit(solution)/shard_map/ppermute | solution.py:152
  745.3 202.6 %collective-permute-start.1 = (bf16[2,1,512,128]{3,2,1,0:T(8,128)(2,1)}, bf16[2,1,512,128]{3,2,1,0:T(8,128)(2,1)}, u32[]{:S(2)}, u32[]{:S(2)}) collective-permute-start(bf16[2,1,512,128]{3,2,1,0:T(8,128)(2,1)} %get-tuple-element.81), channel_id=1, source_target_pairs={{0,3},{1,2},{2,1},{3,0},{4,7},{5,6},{6,5},{7,4}} | collective-permute-start | bytes 786440 | tf_op jit(solution)/shard_map/ppermute | solution.py:152
  747.2 200.7 %collective-permute-start.2 = (bf16[2,1,512,128]{3,2,1,0:T(8,128)(2,1)}, bf16[2,1,512,128]{3,2,1,0:T(8,128)(2,1)}, u32[]{:S(2)}, u32[]{:S(2)}) collective-permute-start(bf16[2,1,512,128]{3,2,1,0:T(8,128)(2,1)} %get-tuple-element.82), channel_id=1, source_target_pairs={{0,1},{1,0},{2,3},{3,2},{4,5},{5,4},{6,7},{7,6}} | collective-permute-start | bytes 786440 | tf_op jit(solution)/shard_map/ppermute | solution.py:152
  792.1 155.7 %collective-permute-start = (bf16[2,1,512,128]{3,2,1,0:T(8,128)(2,1)}, bf16[2,1,512,128]{3,2,1,0:T(8,128)(2,1)}, u32[]{:S(2)}, u32[]{:S(2)}) collective-permute-start(bf16[2,1,512,128]{3,2,1,0:T(8,128)(2,1)} %get-tuple-element.80.token_ref), channel_id=1, source_target_pairs={{0,2},{1,3},{2,0},{3,1},{4,6},{5,7},{6,4},{7,5}} | collective-permute-start | bytes 786440 | tf_op jit(solution)/shard_map/ppermute | solution.py:152
  (42 other events, 3736.4 us)
